TPU v7x, 32 devices: a whole 2x2x4 slice. The times are simulated.
32 devices in a mesh: leaf: 8 (over z, y), sub: 4 (over x, core).
Axes of the slice: x: 2, y: 2, z: 4, core: 2. Of those that a mesh axis runs over, the one named last changes fastest.
Arguments:
- vectors: bfloat16 [64, 8192], P('sub', 'leaf'), may hold values from -6 to 6
- near_blocks: bfloat16 [32, 9, 256, 256], P(('leaf', 'sub')), may hold values from -0.125 to 0.125
- near_cols: int32 [32, 9], P(('leaf', 'sub')), may hold values from 0 to 31, as said below
- near_mask: int32 [32, 9], P(('leaf', 'sub')), may hold values from 0 to 1, as said below
- leaf_basis: bfloat16 [32, 32, 256], P('leaf'), may hold values from -0.375 to 0.375
- transfer: bfloat16 [48, 32, 32], P('leaf'), may hold values from -1 to 1
- coupling: bfloat16 [56, 27, 32, 32], P('leaf'), may hold values from -0.3125 to 0.3125
- far_targets: int32 [56, 27], P('leaf'), may hold values from 0 to 55, as said below
- far_mask: int32 [56, 27], P('leaf'), may hold values from 0 to 1
Outputs:
- result: bfloat16 [64, 8192], P('sub', 'leaf')
Inputs may be any that keep to these rules, and one draw needn't show every extreme that they name: `near_cols`: row i names 9 leaves; its first entry is leaf i; every entry is a leaf of the subtree of leaf i or of the subtree just before or after it; the entries marked live are distinct. `near_mask`: the first entry of each row is 1. `far_targets`: entry (c, k) names a cluster on the same level as cluster c, in any subtree. The 189 entries of one subtree's rows, masked ones included, name clusters of any one subtree at most 32 times; in every draw some subtree is named exactly 32 times, by live entries, from every subtree.
All inputs are finite; a program needn't handle non-finite values.
Results may differ from a plain program's by a relative error of at most 0.0065.
Values may be sent and summed in bfloat16 or wider, within the bound.
A program may use at most 64 MiB of HBM per device.

v0:
```python
import jax
import jax.numpy as jnp
from jax import lax
from jax.sharding import PartitionSpec as P


def with_halo(cells, sides, width):
    for axis, dim in sides:
        count = lax.axis_size(axis)
        ends = count - 1
        head = lax.slice_in_dim(cells, 0, width, axis=dim)
        tail = lax.slice_in_dim(cells, cells.shape[dim] - width, cells.shape[dim], axis=dim)
        cells = jnp.concatenate(
            [
                lax.ppermute(tail, axis, [(i, (i + 1) % count) for i in range(ends)]),
                cells,
                lax.ppermute(head, axis, [((i + 1) % count, i) for i in range(ends)]),
            ],
            axis=dim,
        )
    return cells


def near_field(window, blocks, columns, alive_mask, first_leaf, leaf_size):
    row_count = window.shape[0]
    pieces = window.reshape(row_count, window.shape[1] // leaf_size, leaf_size)
    relative = (columns - first_leaf).reshape(-1)
    taken = jnp.take(pieces, relative, axis=1)
    taken = taken.reshape(row_count, columns.shape[0], columns.shape[1], leaf_size)
    taken = taken * alive_mask.astype(jnp.bfloat16)[None, :, :, None]
    product = jnp.einsum("vjkp,jkpq->vjq", taken, blocks, preferred_element_type=jnp.float32)
    return product.reshape(row_count, columns.shape[0] * leaf_size)


def pack_slots(values, owners, places, peer_count, capacity):
    highest = lax.Precision.HIGHEST
    peer_ids = jnp.arange(peer_count, dtype=jnp.int32)
    onehot = (owners[:, None] == peer_ids[None, :]).astype(jnp.int32)
    rank_within = jnp.sum(onehot * (jnp.cumsum(onehot, axis=0) - 1), axis=1)
    slot_of = owners * capacity + rank_within
    slot_ids = jnp.arange(peer_count * capacity, dtype=jnp.int32)
    select = slot_ids[:, None] == slot_of[None, :]
    send_values = jnp.dot(select.astype(jnp.float32), values, precision=highest)
    send_places = jnp.sum(jnp.where(select, places[None, :], 0), axis=1)
    return (send_values, send_places)


def sum_slots(got_values, got_places, clusters):
    cluster_ids = jnp.arange(clusters, dtype=jnp.int32)
    hits = (got_places[None, :] == cluster_ids[:, None]).astype(jnp.float32)
    return jnp.dot(hits, got_values, precision=lax.Precision.HIGHEST)


def local(
    vectors,
    near_blocks,
    near_cols,
    near_mask,
    leaf_basis,
    transfer,
    coupling,
    far_targets,
    far_mask,
):
    highest = lax.Precision.HIGHEST
    leaf_size = leaf_basis.shape[2]
    subtree = leaf_basis.shape[0]
    clusters = coupling.shape[0]
    far_count = coupling.shape[1]
    rank_size = coupling.shape[2]
    own_vecs = vectors.shape[0]
    peer_count = lax.axis_size("leaf")
    tree_index = lax.axis_index("leaf")
    window_first = (tree_index - 1) * subtree
    padded = with_halo(vectors, (("leaf", 1),), subtree * leaf_size)
    window = lax.all_gather(padded, "sub", axis=0, tiled=True)
    near_part = near_field(window, near_blocks, near_cols, near_mask, window_first, leaf_size)
    near_total = lax.all_to_all(
        near_part.astype(jnp.bfloat16), "sub", split_axis=0, concat_axis=1, tiled=True
    ).astype(near_part.dtype)
    sizes_all = []
    level_size = subtree
    while level_size >= 1:
        sizes_all.append(level_size)
        level_size = level_size // 2
    starts_all = [sum(sizes_all[:number]) for number in range(len(sizes_all))]
    maps_all = transfer.astype(jnp.float32)
    leaf_pieces = vectors.reshape(own_vecs, subtree, leaf_size)
    coeffs = jnp.einsum("vsp,srp->svr", leaf_pieces, leaf_basis, preferred_element_type=jnp.float32)
    hats = [coeffs]
    for level_no in range(len(sizes_all) - 1):
        level_size = sizes_all[level_no]
        level_start = starts_all[level_no]
        child = hats[-1].reshape(level_size // 2, 2, own_vecs, rank_size)
        level_maps = maps_all[level_start : level_start + level_size].reshape(
            level_size // 2, 2, rank_size, rank_size
        )
        hats.append(jnp.einsum("pcvr,pcrq->pvq", child, level_maps, precision=highest))
    all_hats = jnp.concatenate(hats, axis=0)
    terms = jnp.einsum("cvr,ckrq->ckvq", all_hats, coupling.astype(jnp.float32), precision=highest)
    terms = terms * far_mask.astype(jnp.float32)[:, :, None, None]
    terms = terms.reshape(clusters * far_count, own_vecs * rank_size)
    owners = (far_targets // clusters).reshape(-1)
    places = (far_targets % clusters).reshape(-1)
    capacity = max(2, (4 * clusters * far_count + 3 * peer_count - 1) // (3 * peer_count))
    send_values, send_places = pack_slots(terms, owners, places, peer_count, capacity)
    got_values, got_places = (
        lax.all_to_all(send_values, "leaf", split_axis=0, concat_axis=0, tiled=True),
        lax.all_to_all(send_places, "leaf", split_axis=0, concat_axis=0, tiled=True),
    )
    incoming = sum_slots(got_values, got_places, clusters)
    incoming = incoming.reshape(clusters, own_vecs, rank_size)
    downward = [
        incoming[starts_all[number] : starts_all[number] + sizes_all[number]]
        for number in range(len(sizes_all))
    ]
    for level_no in range(len(sizes_all) - 2, -1, -1):
        level_size = sizes_all[level_no]
        level_start = starts_all[level_no]
        level_maps = maps_all[level_start : level_start + level_size].reshape(
            level_size // 2, 2, rank_size, rank_size
        )
        pushed = jnp.einsum("pvq,pcrq->pcvr", downward[level_no + 1], level_maps, precision=highest)
        downward[level_no] = downward[level_no] + pushed.reshape(level_size, own_vecs, rank_size)
    far_out = jnp.einsum(
        "svr,srp->vsp", downward[0], leaf_basis.astype(jnp.float32), precision=highest
    )
    far_out = far_out.reshape(own_vecs, subtree * leaf_size)
    return (near_total + far_out).astype(jnp.bfloat16)


def solution(mesh):
    return jax.shard_map(
        local,
        mesh=mesh,
        in_specs=(
            P("sub", "leaf"),
            P(("leaf", "sub"), None, None, None),
            P(("leaf", "sub"), None),
            P(("leaf", "sub"), None),
            P("leaf", None, None),
            P("leaf", None, None),
            P("leaf", None, None, None),
            P("leaf", None),
            P("leaf", None),
        ),
        out_specs=P("sub", "leaf"),
        check_vma=False,
    )
```

profile of v0, /device:TPU:0, one launch (start us, length us, event | category | flops | bytes accessed | tf_op | source)
XLA Modules:
  0.0 52.0 jit_solution(10137854719792980306)
XLA Ops:
  0.0 0.0 copy-start
  0.0 1.4 %collective-permute-start.1 = (bf16[16,1024]{1,0:T(8,128)(2,1)}, bf16[16,1024]{1,0:T(8,128)(2,1)}, u32[]{:S(2)}, u32[]{:S(2)}) collective-permute-start(bf16[16,1024]{1,0:T(8,128)(2,1)} %param.9), channel_id=1, source_target_pairs={{4,0},{8,4},{12,8},{16,12},{20,16},{24,20},{28,24},{5,1},{9,5},{13... | collective-permute-start | bytes 98312 | tf_op jit(solution)/shard_map/ppermute | solution.py:17
  1.4 6.1 %collective-permute-start = (bf16[16,1024]{1,0:T(8,128)(2,1)}, bf16[16,1024]{1,0:T(8,128)(2,1)}, u32[]{:S(2)}, u32[]{:S(2)}) collective-permute-start(bf16[16,1024]{1,0:T(8,128)(2,1)} %param.9), channel_id=1, source_target_pairs={{0,4},{4,8},{8,12},{12,16},{16,20},{20,24},{24,28},{1,5},{5,9},{9,... | collective-permute-start | bytes 98312 | tf_op jit(solution)/shard_map/ppermute | solution.py:15
  7.6 0.7 %add_select_fusion = (s32[7,27]{1,0:T(8,128)S(1)}, s32[7,27]{1,0:T(8,128)S(1)}) fusion(s32[7,27]{1,0:T(8,128)} %param.16), kind=kLoop, calls=%fused_computation.49 | loop fusion | flops 2268 | bytes 2268 | tf_op jit(solution)/shard_map/jit(remainder)/select_n | solution.py:104
  8.3 0.1 reshape.157
  8.4 0.6 %reduce-window.6 = s32[8,2,128]{2,0,1:T(8,128)S(1)} reduce-window(s32[8,2,128]{2,0,1:T(8,128)S(1)} %convert_bitcast_fusion, s32[]{:T(128)} %constant.49.clone.1), window={size=1x1x128 pad=0_0x0_0x127_0}, to_apply=%region_0.1 | reduce-window | flops 260096 | bytes 16388 | tf_op jit(solution)/shard_map/reduce-window
  9.0 0.2 slice_reduce_fusion
  9.2 0.1 add_bitcast_fusion
  9.3 0.0 copy-start.3
  9.3 0.1 broadcast_in_dim.33
  9.4 0.1 select_reduce_fusion
  9.5 0.7 %all_to_all.21 = s32[8,32,1]{1,0,2:T(8,128)} reshape(s32[256]{0:T(256)S(1)} %select_reduce_fusion) | data formatting | bytes 2048 | tf_op jit(solution)/shard_map/all_to_all | solution.py:109
  10.2 5.6 %all-to-all-start.1 = ((s32[8,32,1]{1,2,0:T(1,128)}), s32[8,32,1]{1,2,0:T(1,128)}, u32[]{:S(2)}, u32[]{:S(2)}) async-start(s32[8,32,1]{1,2,0:T(1,128)} %bitcast.14), calls=%async_computation.1 | async-start | bytes 8192 | tf_op jit(solution)/shard_map/all_to_all | solution.py:109
  15.8 0.6 %multiply_add_fusion = s32[8,32]{1,0:T(8,128)} fusion(), kind=kLoop, calls=%fused_computation.52 | loop fusion | flops 512 | bytes 1024 | tf_op jit(solution)/shard_map/eq | solution.py:42
  16.4 0.7 %convert_element_type.50 = f32[7,27]{1,0:T(8,128)S(1)} convert(s32[7,27]{1,0:T(8,128)} %param.17) | non-fusion elementwise | flops 189 | bytes 1512 | tf_op jit(solution)/shard_map/convert_element_type | solution.py:101
  17.1 0.8 %slice.36 = bf16[4,32,32]{2,1,0:T(8,128)(2,1)S(1)} slice(bf16[6,32,32]{2,1,0:T(8,128)(2,1)} %param.14), slice={[0:4], [0:32], [0:32]} | slice | bytes 16384 | tf_op jit(solution)/shard_map/slice | solution.py:95
  17.9 1.0 %fusion.26 = f32[4,16,32]{2,1,0:T(8,128)S(1)} fusion(bf16[4,32,256]{2,1,0:T(8,128)(2,1)} %param.13, bf16[2,4,8,256]{3,2,1,0:T(8,128)(2,1)} %bitcast.105), kind=kOutput, calls=%fused_computation.33 | convolution fusion | flops 1048576 | bytes 106496 | tf_op jit(solution)/shard_map/vsp,srp->svr/dot_general | solution.py:89
  18.9 0.2 convolution_bitcast_fusion.1
  19.1 0.9 %convolution_bitcast_fusion.2 = f32[1,16,32]{2,1,0:T(8,128)S(1)} fusion(f32[2,16,32]{2,1,0:T(8,128)S(1)} %convolution_bitcast_fusion.1, bf16[6,32,32]{2,1,0:T(8,128)(2,1)} %param.14), kind=kOutput, calls=%fused_computation.13 | convolution fusion | flops 393216 | bytes 22528 | tf_op jit(solution)/shard_map/pcvr,pcrq->pvq/dot_general | solution.py:98
  20.0 0.0 copy-done.3
  20.0 0.0 copy-done
  20.0 0.8 %multiply_bitcast_fusion = f32[7,27,16,32]{3,2,1,0:T(8,128)S(1)} fusion(bf16[7,27,32,32]{3,2,1,0:T(8,128)(2,1)S(1)} %copy-done, f32[7,27]{1,0:T(8,128)S(1)} %convert_element_type.50, f32[1,16,32]{2,1,0:T(8,128)S(1)} %convolution_bitcast_fusion.2, f32[2,16,32]{2,1,0:T(8,128)S(1)} %convolution_bitcast_fusion.1, f32[4,16,32]{2,1,0:T(8,128)S(1)} %fusion.26), kind=kOutput, calls=%fused_computation.1 | convolution fusion | flops 37262848 | bytes 789236 | tf_op jit(solution)/shard_map/cvr,ckrq->ckvq/dot_general | solution.py:100
  20.8 0.0 copy-start.2
  20.9 0.6 %reshape.180 = f32[189,512,1]{1,0,2:T(8,128)S(1)} reshape(f32[7,27,16,32]{3,2,1,0:T(8,128)S(1)} %multiply_bitcast_fusion) | data formatting | bytes 774144 | tf_op jit(solution)/shard_map/reshape | solution.py:102
  21.4 0.0 copy-start.4
  21.5 1.9 %fusion.16 = f32[8,32,512]{2,1,0:T(8,128)} fusion(f32[189,512,1]{1,0,2:T(8,128)S(1)} %reshape.180, s32[189]{0:T(256)} %copy-done.3, s32[8,32]{1,0:T(8,128)} %multiply_add_fusion), kind=kOutput, calls=%fused_computation.19 | convolution fusion | flops 297319680 | bytes 913140 | tf_op jit(solution)/shard_map/dot_general | solution.py:43
  23.4 0.7 %fusion.36 = s32[9]{0:T(128)S(1)} fusion(s32[1,9]{1,0:T(1,128)} %param.11, s32[]{:T(128)S(6)} %mul.40), kind=kLoop, calls=%fused_computation.62 | loop fusion | flops 36 | bytes 76 | tf_op jit(solution)/shard_map/jit(_take)/jit(_where)/select_n | solution.py:28
  24.0 0.7 %compare_and_fusion = pred[9]{0:T(512)(128)(4,1)S(1)} fusion(s32[1,9]{1,0:T(1,128)} %param.11, s32[]{:T(128)S(6)} %mul.40), kind=kLoop, calls=%fused_computation.60 | loop fusion | flops 63 | bytes 49 | tf_op jit(solution)/shard_map/jit(_take)/and | solution.py:28
  24.7 0.0 all-to-all-done.1
  24.7 6.0 %all-to-all-start.2 = ((f32[8,32,512]{2,1,0:T(8,128)}), f32[8,32,512]{2,1,0:T(8,128)S(1)}, u32[]{:S(2)}, u32[]{:S(2)}) async-start(f32[8,32,512]{2,1,0:T(8,128)} %fusion.16), calls=%async_computation.2 | async-start | bytes 1048576 | tf_op jit(solution)/shard_map/all_to_all | solution.py:108
  30.7 0.0 copy-done.4
  30.7 0.5 broadcast.118
  31.2 1.3 %reduce.9 = s32[8,32]{1,0:T(8,128)S(1)} reduce(s32[8,32,1]{1,2,0:T(1,128)} %all-to-all-done.1, s32[]{:T(128)} %broadcast.118), dimensions={2}, to_apply=%all_to_all.22.reduce_sub_computation.3 | reduce | bytes 2052 | tf_op jit(solution)/shard_map/all_to_all | solution.py:109
  32.6 0.1 eq.76
  32.7 0.0 collective-permute-done.1
  32.7 0.0 collective-permute-done
  32.7 0.0 copy-done.2
  32.7 0.8 %pad_maximum_fusion = bf16[16,3072]{1,0:T(8,128)(2,1)S(1)} fusion(bf16[16,1024]{1,0:T(8,128)(2,1)} %collective-permute-done.1, bf16[16,1024]{1,0:T(8,128)(2,1)S(1)} %copy-done.2, bf16[16,1024]{1,0:T(8,128)(2,1)} %collective-permute-done), kind=kLoop, calls=%fused_computation.27 | loop fusion | flops 294912 | bytes 196608 | tf_op jit(solution)/shard_map/concatenate | solution.py:13
  33.5 6.4 %all_gather.3 = bf16[64,3072]{1,0:T(8,128)(2,1)S(1)} all-gather(bf16[16,3072]{1,0:T(8,128)(2,1)S(1)} %pad_maximum_fusion), channel_id=1, replica_groups=mesh['leaf'=8,'sub'=4] {'sub'}, dimensions={0}, use_global_device_ids=true | all-gather | bytes 491520 | tf_op jit(solution)/shard_map/all_gather | solution.py:76
  39.9 0.0 copy-start.1
  39.9 0.6 %gather_fusion = bf16[9,64,256]{2,1,0:T(8,128)(2,1)S(1)} fusion(bf16[64,12,256]{2,0,1:T(8,128)(2,1)S(1)} %bitcast.99, s32[1024]{0:T(1024)S(1)} %pad_clamp_fusion), kind=kCustom, calls=%fused_computation | custom fusion | bytes 589860 | tf_op jit(solution)/shard_map/jit(_take)/gather | solution.py:28
  40.5 2.3 %fusion.5 = bf16[64,256]{1,0:T(8,128)(2,1)} fusion(bf16[1,9,256,256]{3,2,1,0:T(8,128)(2,1)} %param.10, bf16[9,64,256]{2,1,0:T(8,128)(2,1)S(1)} %gather_fusion, pred[9]{0:T(512)(128)(4,1)S(1)} %compare_and_fusion, bf16[9]{0:T(256)(128)(2,1)S(1)} %convert_bitcast_fusion.1), kind=kOutput, calls=%fused_computation.6 | convolution fusion | flops 75808768 | bytes 1507355 | tf_op jit(solution)/shard_map/vjkp,jkpq->vjq/dot_general | solution.py:31
  42.8 1.3 %all-to-all-done.2 = f32[8,32,512]{2,1,0:T(8,128)S(1)} async-done(((f32[8,32,512]{2,1,0:T(8,128)}), f32[8,32,512]{2,1,0:T(8,128)S(1)}, u32[]{:S(2)}, u32[]{:S(2)}) %all-to-all-start.2) | async-done | bytes 524320 | tf_op jit(solution)/shard_map/all_to_all | solution.py:108
  44.1 3.3 %all-to-all-start = ((bf16[4,16,256]{2,1,0:T(8,128)(2,1)}), bf16[4,16,256]{2,1,0:T(8,128)(2,1)S(1)}, u32[]{:S(2)}, u32[]{:S(2)}) async-start(bf16[4,16,256]{2,1,0:T(8,128)(2,1)} %bitcast.10), calls=%async_computation | async-start | bytes 65536 | tf_op jit(solution)/shard_map/all_to_all | solution.py:78
  47.3 0.3 fusion.33
  47.6 0.1 slice.39
  47.7 0.1 slice.41
  47.8 0.1 reshape.181
  47.9 0.9 %fusion.11 = f32[2,16,32,1]{2,1,3,0:T(8,128)S(1)} fusion(f32[2,16,32]{2,1,0:T(8,128)S(1)} %slice.41, f32[16,32,1]{1,0,2:T(8,128)S(1)} %reshape.181, bf16[6,32,32]{2,1,0:T(8,128)(2,1)} %param.14), kind=kOutput, calls=%fused_computation.11 | convolution fusion | flops 394240 | bytes 26624 | tf_op jit(solution)/shard_map/pvq,pcrq->pcvr/dot_general | solution.py:123
  48.8 0.3 fusion.39
  49.1 2.2 %all-to-all-done = bf16[4,16,256]{2,1,0:T(8,128)(2,1)S(1)} async-done(((bf16[4,16,256]{2,1,0:T(8,128)(2,1)}), bf16[4,16,256]{2,1,0:T(8,128)(2,1)S(1)}, u32[]{:S(2)}, u32[]{:S(2)}) %all-to-all-start) | async-done | bytes 32800 | tf_op jit(solution)/shard_map/all_to_all | solution.py:78
  51.2 0.0 copy-done.1
  51.2 0.2 fusion.9
  51.4 0.6 %copy.27 = bf16[4,2,8,256]{3,2,0,1:T(8,128)(2,1)} copy(bf16[4,2,8,256]{3,2,1,0:T(8,128)(2,1)S(1)} %fusion.9) | data formatting | bytes 65536 | tf_op jit(solution)/shard_map/convert_element_type | solution.py:129
  (13 shorter events, 0.2 us)
Async XLA Ops:
  0.0 20.0 %copy-start = (bf16[7,27,32,32]{3,2,1,0:T(8,128)(2,1)S(1)}, bf16[7,27,32,32]{3,2,1,0:T(8,128)(2,1)}, u32[]{:S(2)}) copy-start(bf16[7,27,32,32]{3,2,1,0:T(8,128)(2,1)} %param.15) | copy-start | bytes 1161220
  0.0 32.7 %collective-permute-start.1 = (bf16[16,1024]{1,0:T(8,128)(2,1)}, bf16[16,1024]{1,0:T(8,128)(2,1)}, u32[]{:S(2)}, u32[]{:S(2)}) collective-permute-start(bf16[16,1024]{1,0:T(8,128)(2,1)} %param.9), channel_id=1, source_target_pairs={{4,0},{8,4},{12,8},{16,12},{20,16},{24,20},{28,24},{5,1},{9,5},{13... | collective-permute-start | bytes 98312 | tf_op jit(solution)/shard_map/ppermute | solution.py:17
  1.4 31.2 %collective-permute-start = (bf16[16,1024]{1,0:T(8,128)(2,1)}, bf16[16,1024]{1,0:T(8,128)(2,1)}, u32[]{:S(2)}, u32[]{:S(2)}) collective-permute-start(bf16[16,1024]{1,0:T(8,128)(2,1)} %param.9), channel_id=1, source_target_pairs={{0,4},{4,8},{8,12},{12,16},{16,20},{20,24},{24,28},{1,5},{5,9},{9,... | collective-permute-start | bytes 98312 | tf_op jit(solution)/shard_map/ppermute | solution.py:15
  9.3 10.7 %copy-start.3 = (s32[189]{0:T(256)}, s32[189]{0:T(256)S(1)}, u32[]{:S(2)}) copy-start(s32[189]{0:T(256)S(1)} %multiply_add_fusion.1) | copy-start | bytes 2272
  10.2 14.5 %all-to-all-start.1 = ((s32[8,32,1]{1,2,0:T(1,128)}), s32[8,32,1]{1,2,0:T(1,128)}, u32[]{:S(2)}, u32[]{:S(2)}) async-start(s32[8,32,1]{1,2,0:T(1,128)} %bitcast.14), calls=%async_computation.1 | async-start | bytes 8192 | tf_op jit(solution)/shard_map/all_to_all | solution.py:109
  20.8 11.8 %copy-start.2 = (bf16[16,1024]{1,0:T(8,128)(2,1)S(1)}, bf16[16,1024]{1,0:T(8,128)(2,1)}, u32[]{:S(2)}) copy-start(bf16[16,1024]{1,0:T(8,128)(2,1)} %param.9) | copy-start | bytes 98308
  21.4 9.2 %copy-start.4 = (s32[1,9]{1,0:T(1,128)S(1)}, s32[1,9]{1,0:T(1,128)}, u32[]{:S(2)}) copy-start(s32[1,9]{1,0:T(1,128)} %param.12) | copy-start | bytes 112
  24.7 19.4 %all-to-all-start.2 = ((f32[8,32,512]{2,1,0:T(8,128)}), f32[8,32,512]{2,1,0:T(8,128)S(1)}, u32[]{:S(2)}, u32[]{:S(2)}) async-start(f32[8,32,512]{2,1,0:T(8,128)} %fusion.16), calls=%async_computation.2 | async-start | bytes 1048576 | tf_op jit(solution)/shard_map/all_to_all | solution.py:108
  39.9 11.3 %copy-start.1 = (bf16[4,32,256]{2,1,0:T(8,128)(2,1)S(1)}, bf16[4,32,256]{2,1,0:T(8,128)(2,1)}, u32[]{:S(2)}) copy-start(bf16[4,32,256]{2,1,0:T(8,128)(2,1)} %param.13) | copy-start | bytes 196612
  44.1 7.2 %all-to-all-start = ((bf16[4,16,256]{2,1,0:T(8,128)(2,1)}), bf16[4,16,256]{2,1,0:T(8,128)(2,1)S(1)}, u32[]{:S(2)}, u32[]{:S(2)}) async-start(bf16[4,16,256]{2,1,0:T(8,128)(2,1)} %bitcast.10), calls=%async_computation | async-start | bytes 65536 | tf_op jit(solution)/shard_map/all_to_all | solution.py:78
where the time goes:
time: 52.9 us; the launch traced here: 52 us
  starting transfers between devices  22.4 us (42%)
  matrix products  8.67 us (16%)
  blocking collectives  6.44 us (12%)
  other arithmetic  6.36 us (12%)
  local copies, waits for them, and re-layouts  4.48 us (8%)
  waiting for transfers between devices  3.43 us (6%)
    all_gather x1, blocking collectives, local(): window = lax.all_gather(padded, 'sub', axis=0, tiled=True)  6.44 us
    ppermute x1, starting transfers between devices, with_halo(): lax.ppermute(tail, axis, [(i, (i + 1) % count) for i in range(ends)])  6.14 us
    all_to_all x1, starting transfers between devices, local(): lax.all_to_all(send_values, 'leaf', split_axis=0, concat_axis=0, tiled=True)  6 us
    all_to_all x1, starting transfers between devices, local(): lax.all_to_all(send_places, 'leaf', split_axis=0, concat_axis=0, tiled=True)  5.62 us
    all_to_all x1, starting transfers between devices, local(): lax.all_to_all(near_part.astype(jnp.bfloat16), 'sub', split_axis=0, conca...  3.26 us
    dot_general x1, matrix products, near_field(): jnp.einsum('vjkp,jkpq->vjq', taken, blocks, preferred_element_type=jnp.fl...  2.28 us
    all_to_all x1, waiting for transfers between devices, local(): lax.all_to_all(near_part.astype(jnp.bfloat16), 'sub', split_axis=0, conca...  2.17 us
    dot_general x1, matrix products, pack_slots(): send_values = jnp.dot(select.astype(jnp.float32), values, precision=highest)  1.9 us
  transfers between devices with their start and end apart: 5, of which 2 were waited for; matrix products, arithmetic and copies ran while one was open for 35% of the time, Pallas kernels for 0%

commit v1 on v0

v1 whole, which is shorter than its diff:
```python
import functools

import jax
import jax.numpy as jnp
from jax import lax
from jax.experimental import pallas as pl
from jax.experimental.pallas import tpu as pltpu
from jax.sharding import PartitionSpec as P

F32 = jnp.float32
BF16 = jnp.bfloat16
MESH = pl.DeviceIdType.MESH


def mm(a, b):
    return lax.dot_general(a, b, (((1,), (0,)), ((), ())), preferred_element_type=F32)


def nt(a, b):
    return lax.dot_general(a, b, (((1,), (1,)), ((), ())), preferred_element_type=F32)


def iota(shape, dim):
    return lax.broadcasted_iota(jnp.int32, shape, dim)


def quo(x, n):
    if n & (n - 1) == 0:
        return lax.shift_right_logical(x, jnp.int32(n.bit_length() - 1))
    return lax.div(x, jnp.int32(n))


def same(a, b):
    return jnp.where(a == b, 1.0, 0.0).astype(BF16)


def levels_of(subtree):
    found = []
    start = 0
    size = subtree
    while size >= 1:
        found.append((start, size))
        start += size
        size //= 2
    return found


def kernel(
    dims,
    vec_hbm,
    nb_hbm,
    cols_ref,
    live_ref,
    basis_hbm,
    trans_hbm,
    coup_hbm,
    tgt_hbm,
    fmask_hbm,
    out_ref,
    win,
    nb,
    basis,
    trans,
    coup,
    tgt,
    fmask,
    rmat,
    fsend,
    frecv,
    nsend,
    nrecv,
    ld_sem,
    w_send,
    w_recv,
    h_send,
    f_send,
    f_recv,
    n_send,
    n_recv,
):
    trees, subs, pair, chunk = dims
    groups = subs // pair
    own, subtree, leaf = vec_hbm.shape[0], basis.shape[0], basis.shape[2]
    clusters, far, rank = coup.shape[0], coup.shape[1], coup.shape[2]
    near = nb.shape[0]
    levels = levels_of(subtree)
    tree = lax.axis_index("leaf")
    sub = lax.axis_index("sub")
    group, core = lax.div(sub, jnp.int32(pair)), lax.rem(sub, jnp.int32(pair))
    has = (tree > 0, None, tree < trees - 1)
    goes = (tree < trees - 1, None, tree > 0)

    def guarded(cond, action):
        if cond is None:
            action()
        else:
            pl.when(cond)(action)

    loads = [
        pltpu.make_async_copy(vec_hbm, win.at[1, sub], ld_sem.at[0]),
        pltpu.make_async_copy(basis_hbm, basis, ld_sem.at[1]),
        pltpu.make_async_copy(trans_hbm, trans, ld_sem.at[2]),
        pltpu.make_async_copy(tgt_hbm, tgt, ld_sem.at[3]),
        pltpu.make_async_copy(fmask_hbm, fmask, ld_sem.at[4]),
        pltpu.make_async_copy(coup_hbm, coup, ld_sem.at[5]),
        pltpu.make_async_copy(nb_hbm.at[0], nb, ld_sem.at[6]),
    ]
    for load in loads:
        load.start()

    barrier = pltpu.get_barrier_semaphore()

    def greet(to_tree, to_sub):
        pl.semaphore_signal(barrier, inc=1, device_id=(to_tree, to_sub), device_id_type=MESH)

    def other(step):
        return lax.rem(group + step, jnp.int32(groups)) * pair + core

    def greet_tree(step, carry):
        greet(lax.rem(tree + step, jnp.int32(trees)), sub)
        return carry

    lax.fori_loop(1, trees, greet_tree, 0, unroll=trees <= 16)
    for step in range(1, subs):
        greet(tree, lax.rem(sub + step, jnp.int32(subs)))
    for slot in (0, 2):
        for step in range(1, groups):
            guarded(
                goes[slot],
                functools.partial(lambda sl, st: greet(tree + 1 - sl, other(st)), slot, step),
            )
    greeted = (trees - 1) + (subs - 1)
    sides = goes[0].astype(jnp.int32) + goes[2].astype(jnp.int32)

    for slot in (0, 2):
        @pl.when(jnp.logical_not(has[slot]))
        def _():
            win[slot] = jnp.zeros(win.shape[1:], win.dtype)

    loads[0].wait()
    pl.semaphore_wait(barrier, greeted + (groups - 1) * sides)

    def spread(slot, step):
        return pltpu.make_async_remote_copy(
            src_ref=win.at[1, sub],
            dst_ref=win.at[slot, sub],
            send_sem=w_send.at[slot, step],
            recv_sem=w_recv.at[slot, sub],
            device_id=(tree + 1 - slot, other(step)),
            device_id_type=MESH,
        )

    def arrived(slot, from_sub):
        pltpu.make_async_remote_copy(
            src_ref=win.at[slot, from_sub],
            dst_ref=win.at[slot, from_sub],
            send_sem=w_send.at[slot, 0],
            recv_sem=w_recv.at[slot, from_sub],
            device_id=(tree, sub),
            device_id_type=MESH,
        ).wait_recv()

    def hand_over(slot, step, core_step):
        held = other(step)
        return pltpu.make_async_remote_copy(
            src_ref=win.at[slot, held],
            dst_ref=win.at[slot, held],
            send_sem=h_send.at[slot, step, core_step],
            recv_sem=w_recv.at[slot, held],
            device_id=(tree, group * pair + lax.rem(core + core_step, jnp.int32(pair))),
            device_id_type=MESH,
        )

    first_hops = [(slot, step) for step in range(groups) for slot in (0, 2, 1) if (slot, step) != (1, 0)]
    for slot, step in first_hops:
        guarded(goes[slot], functools.partial(lambda a, b: spread(a, b).start(), slot, step))
    for core_step in range(1, pair):
        hand_over(1, 0, core_step).start()

    for load in loads[1:6]:
        load.wait()
    ups = []
    for s in range(subtree):
        piece = win[1, sub, :, s * leaf : (s + 1) * leaf]
        ups.append(nt(piece, basis[s]).astype(BF16))
    for number in range(len(levels) - 1):
        start, size = levels[number]
        for parent in range(size // 2):
            kid = start + 2 * parent
            ups.append((mm(ups[kid], trans[kid]) + mm(ups[kid + 1], trans[kid + 1])).astype(BF16))

    wide = far * rank
    targets = tgt[...]
    owner = jnp.floor((targets.astype(F32) + 0.5) * (1.0 / clusters)).astype(jnp.int32)
    place = targets - owner * clusters
    owner = jnp.where(fmask[...] > 0, owner, -1)
    spread_k = same(quo(iota((far, wide), 1), rank), iota((far, wide), 0))
    spread_rows = same(quo(iota((wide, far), 0), rank), iota((wide, far), 1))
    tile_wide = same(iota((rank, wide), 1) & (rank - 1), iota((rank, wide), 0))
    for start, size in levels:
        width = size * rank
        tile = same(iota((rank, width), 1) & (rank - 1), iota((rank, width), 0))
        for c in range(start, start + size):
            tiled = mm(coup[c].reshape(wide, rank), tile)
            picks = same(quo(iota((width, far), 0), rank) + start, place[c : c + 1, :])
            chosen = nt(spread_rows, picks)
            rmat[c, :, :width] = (tiled * chosen).astype(BF16)
    up_wide = [mm(up, tile_wide) for up in ups]

    def couple(number, carry):
        base = number * chunk
        sums = []
        for start, size in levels:
            total = None
            for c in range(start, start + size):
                mine = same(quo(iota((chunk * own, far), 0), own) + base, owner[c : c + 1, :])
                left = mm(mine, spread_k) * jnp.concatenate([up_wide[c]] * chunk, axis=0)
                term = mm(left.astype(BF16), rmat[c, :, : size * rank])
                total = term if total is None else total + term
            sums.append(total)
        spare = fsend.shape[2] - clusters * rank
        if spare:
            sums.append(jnp.zeros((chunk * own, spare), F32))
        joined = jnp.concatenate(sums, axis=1).astype(BF16)
        fsend[pl.ds(base, chunk)] = joined.reshape(chunk, own, fsend.shape[2])
        return carry

    lax.fori_loop(0, trees // chunk, couple, 0, unroll=trees == chunk)

    def far_copy(step):
        to = lax.rem(tree + step, jnp.int32(trees))
        return pltpu.make_async_remote_copy(
            src_ref=fsend.at[to],
            dst_ref=frecv.at[tree],
            send_sem=f_send.at[to],
            recv_sem=f_recv.at[tree],
            device_id=(to, sub),
            device_id_type=MESH,
        )

    def far_arrived(step):
        source = lax.rem(tree + step, jnp.int32(trees))
        pltpu.make_async_remote_copy(
            src_ref=fsend.at[source],
            dst_ref=frecv.at[source],
            send_sem=f_send.at[source],
            recv_sem=f_recv.at[source],
            device_id=(source, sub),
            device_id_type=MESH,
        ).wait_recv()
        return source

    def start_far(step, carry):
        far_copy(step).start()
        return carry

    lax.fori_loop(1, trees, start_far, 0, unroll=trees <= 16)

    loads[6].wait()
    total = jnp.zeros((subs * own, leaf), F32)

    def relay(slot, step):
        arrived(slot, other(step))
        for core_step in range(1, pair):
            hand_over(slot, step, core_step).start()

    def take(slot, step, core_step):
        from_core = lax.rem(core + core_step, jnp.int32(pair))
        arrived(slot, lax.rem(group + step, jnp.int32(groups)) * pair + from_core)

    for slot, step in [(1, step) for step in range(1, groups)] + [
        (slot, step) for step in range(groups) for slot in (0, 2)
    ]:
        guarded(has[slot], functools.partial(relay, slot, step))

    for slot in (1, 0, 2):
        for step in range(groups):
            for core_step in range(1, pair):
                guarded(has[slot], functools.partial(take, slot, step, core_step))
        for q in range(subtree):
            wanted = (tree + slot - 1) * subtree + q
            index = jnp.int32(0)
            alive = jnp.int32(0)
            for k in range(near):
                hit = jnp.where(cols_ref[0, k] == wanted, live_ref[0, k], 0)
                index = index + hit * k
                alive = alive + hit
            piece = win[slot, :, :, q * leaf : (q + 1) * leaf].reshape(subs * own, leaf)
            total = total + mm(piece, nb[index]) * alive.astype(F32)

    parts = total.reshape(subs, own, leaf).astype(BF16)
    nsend[...] = parts
    nrecv[sub] = nsend[sub]

    def near_copy(step):
        to = lax.rem(sub + step, jnp.int32(subs))
        return pltpu.make_async_remote_copy(
            src_ref=nsend.at[to],
            dst_ref=nrecv.at[sub],
            send_sem=n_send.at[to],
            recv_sem=n_recv.at[sub],
            device_id=(tree, to),
            device_id_type=MESH,
        )

    def near_arrived(step):
        source = lax.rem(sub + step, jnp.int32(subs))
        pltpu.make_async_remote_copy(
            src_ref=nsend.at[source],
            dst_ref=nrecv.at[source],
            send_sem=n_send.at[source],
            recv_sem=n_recv.at[source],
            device_id=(tree, source),
            device_id_type=MESH,
        ).wait_recv()

    for step in range(1, subs):
        near_copy(step).start()

    def add_far(step, carry):
        return carry + frecv[far_arrived(step)].astype(F32)

    incoming = lax.fori_loop(1, trees, add_far, fsend[tree].astype(F32), unroll=trees <= 16)
    downs = incoming[:, levels[-1][0] * rank : clusters * rank]
    for number in range(len(levels) - 2, -1, -1):
        start, size = levels[number]
        pushed = []
        for parent in range(size // 2):
            maps = trans[start + 2 * parent : start + 2 * parent + 2].reshape(2 * rank, rank)
            pushed.append(nt(downs[:, parent * rank : (parent + 1) * rank].astype(BF16), maps))
        pushed = pushed[0] if len(pushed) == 1 else jnp.concatenate(pushed, axis=1)
        downs = incoming[:, start * rank : (start + size) * rank] + pushed
    fars = [
        mm(downs[:, s * rank : (s + 1) * rank].astype(BF16), basis[s]) for s in range(subtree)
    ]

    for step in range(1, subs):
        near_arrived(step)
    for s in range(subtree):
        out_ref[:, s * leaf : (s + 1) * leaf] = (nrecv[s].astype(F32) + fars[s]).astype(BF16)

    for slot, step in first_hops:
        guarded(goes[slot], functools.partial(lambda a, b: spread(a, b).wait_send(), slot, step))
    for slot in range(3):
        for step in range(groups):
            for core_step in range(1, pair):
                guarded(
                    has[slot],
                    functools.partial(lambda *at: hand_over(*at).wait_send(), slot, step, core_step),
                )

    def end_far(step, carry):
        far_copy(step).wait_send()
        return carry

    lax.fori_loop(1, trees, end_far, 0, unroll=trees <= 16)
    for step in range(1, subs):
        near_copy(step).wait_send()


def local(vectors, near_blocks, near_cols, near_mask, leaf_basis, transfer, coupling, far_targets, far_mask):
    trees, subs = lax.axis_size("leaf"), lax.axis_size("sub")
    pair = 2 if subs % 2 == 0 else 1
    groups = subs // pair
    chunk = 8 if trees % 8 == 0 else trees
    own, points = vectors.shape
    clusters, far, rank = coupling.shape[:3]
    leaf = leaf_basis.shape[2]
    lanes = -(-clusters * rank // 128) * 128
    any_spec = pl.BlockSpec(memory_space=pl.ANY)
    smem = pl.BlockSpec(memory_space=pltpu.SMEM)
    dma = pltpu.SemaphoreType.DMA
    return pl.pallas_call(
        functools.partial(kernel, (trees, subs, pair, chunk)),
        out_shape=jax.ShapeDtypeStruct((own, points), BF16),
        in_specs=[any_spec, any_spec, smem, smem] + [any_spec] * 5,
        out_specs=pl.BlockSpec(memory_space=pltpu.VMEM),
        scratch_shapes=[
            pltpu.VMEM((3, subs, own, points), BF16),
            pltpu.VMEM(near_blocks.shape[1:], BF16),
            pltpu.VMEM(leaf_basis.shape, BF16),
            pltpu.VMEM(transfer.shape, BF16),
            pltpu.VMEM(coupling.shape, BF16),
            pltpu.VMEM(far_targets.shape, jnp.int32),
            pltpu.VMEM(far_mask.shape, jnp.int32),
            pltpu.VMEM((clusters, far * rank, leaf_basis.shape[0] * rank), BF16),
            pltpu.VMEM((trees, own, lanes), BF16),
            pltpu.VMEM((trees, own, lanes), BF16),
            pltpu.VMEM((subs, own, leaf), BF16),
            pltpu.VMEM((subs, own, leaf), BF16),
            dma((7,)),
            dma((3, groups)),
            dma((3, subs)),
            dma((3, groups, pair)),
            dma((trees,)),
            dma((trees,)),
            dma((subs,)),
            dma((subs,)),
        ],
        compiler_params=pltpu.CompilerParams(collective_id=0, has_side_effects=True),
    )(vectors, near_blocks, near_cols, near_mask, leaf_basis, transfer, coupling, far_targets, far_mask)


def solution(mesh):
    return jax.shard_map(
        local,
        mesh=mesh,
        in_specs=(
            P("sub", "leaf"),
            P(("leaf", "sub"), None, None, None),
            P(("leaf", "sub"), None),
            P(("leaf", "sub"), None),
            P("leaf", None, None),
            P("leaf", None, None),
            P("leaf", None, None, None),
            P("leaf", None),
            P("leaf", None),
        ),
        out_specs=P("sub", "leaf"),
        check_vma=False,
    )
```

time: 52.9 us -> 16.9 us (0.32); the launches traced: 52 us -> 16.7 us
  starting transfers between devices: 22.4 us -> 0 us
  Pallas kernels: 0 us -> 15.4 us
  matrix products: 8.67 us -> 0 us
  blocking collectives: 6.44 us -> 0 us
  other arithmetic: 6.36 us -> 0 us
  waiting for transfers between devices: 3.43 us -> 0 us
  local copies, waits for them, and re-layouts: 4.48 us -> 1.38 us
    pallas_call x0 -> x1, Pallas kernels: none -> 15.4 us  [local(): pl.pallas_call(functools.partial(kernel, (trees, subs, pair, chunk)), out...]
    all_to_all x3 -> x0, starting transfers between devices: 14.9 us -> none  [the longest x1 6 us: local(): lax.all_to_all(send_values, 'leaf', split_axis=0, concat_axis=0, tiled=True)]
    dot_general x10 -> x0, matrix products: 8.67 us -> none  [the longest x1 2.28 us: near_field(): jnp.einsum('vjkp,jkpq->vjq', taken, blocks, preferred_element_type=jnp.fl...]
    ppermute x2 -> x0, starting transfers between devices: 7.55 us -> none  [the longest x1 6.14 us: with_halo(): lax.ppermute(tail, axis, [(i, (i + 1) % count) for i in range(ends)])]
    all_gather x1 -> x0, blocking collectives: 6.44 us -> none  [local(): window = lax.all_gather(padded, 'sub', axis=0, tiled=True)]
    all_to_all x3 -> x0, waiting for transfers between devices: 3.42 us -> none  [the longest x1 2.17 us: local(): lax.all_to_all(near_part.astype(jnp.bfloat16), 'sub', split_axis=0, conca...]
    select_n x2 -> x0, other arithmetic: 1.36 us -> none  [the longest x1 0.7 us: local(): places = (far_targets % clusters).reshape(-1)]
    unnamed x10 -> x1, local copies, waits for them, and re-layouts: 0.03 us -> 1.38 us
  transfers between devices with their start and end apart: 5 -> 0, of which waited for: 2 -> 0; matrix products, arithmetic and copies ran while one was open for 35% -> 0% of each run, Pallas kernels for 0% -> 0%
where the time goes in v1:
time: 16.9 us; the launch traced here: 16.7 us
  Pallas kernels  15.4 us (91%)
  local copies, waits for them, and re-layouts  1.38 us (8%)
    pallas_call x1, Pallas kernels, local(): pl.pallas_call(functools.partial(kernel, (trees, subs, pair, chunk)), out...  15.4 us
    unnamed x1, local copies, waits for them, and re-layouts  1.38 us

profile of v1, /device:TPU:0, one launch (start us, length us, event | category | flops | bytes accessed | tf_op | source)
XLA Modules:
  0.0 16.7 jit_solution(2951447377622097292)
XLA Ops:
  0.0 15.4 %shard_map.91 = bf16[16,1024]{1,0:T(8,128)(2,1)} custom-call(bf16[16,1024]{1,0:T(8,128)(2,1)} %vec_hbm.1, bf16[1,9,256,256]{3,2,1,0:T(8,128)(2,1)} %nb_hbm.1, s32[1,9]{1,0:T(1,128)} %cols_ref.1, s32[1,9]{1,0:T(1,128)} %live_ref.1, bf16[4,32,256]{2,1,0:T(8,128)(2,1)} %basis_hbm.1, bf16[6,32,32]{2,1,0:T(8,128)(2,1)} %trans_hbm.1, ...), custom_call_target="tpu_custom_call" | custom-call | tf_op jit(solution)/shard_map/pallas_call | solution.py:373
  15.4 1.4 %copy.11 = bf16[16,1024]{1,0:T(8,128)(2,1)} copy(bf16[16,1024]{1,0:T(8,128)(2,1)} %shard_map.91) | data formatting | bytes 65536

commit v2 on v1

--- a/solution.py
+++ b/solution.py
@@ -59,6 +59,8 @@
     out_ref,
     win,
     nb,
+    wown,
+    wpeer,
     basis,
     trans,
     coup,
@@ -69,10 +71,12 @@
     frecv,
     nsend,
     nrecv,
+    known,
     ld_sem,
     w_send,
     w_recv,
     h_send,
+    h_recv,
     f_send,
     f_recv,
     n_send,
@@ -97,7 +101,7 @@
             pl.when(cond)(action)
 
     loads = [
-        pltpu.make_async_copy(vec_hbm, win.at[1, sub], ld_sem.at[0]),
+        pltpu.make_async_copy(vec_hbm, win.at[1, group], ld_sem.at[0]),
         pltpu.make_async_copy(basis_hbm, basis, ld_sem.at[1]),
         pltpu.make_async_copy(trans_hbm, trans, ld_sem.at[2]),
         pltpu.make_async_copy(tgt_hbm, tgt, ld_sem.at[3]),
@@ -105,8 +109,8 @@
         pltpu.make_async_copy(coup_hbm, coup, ld_sem.at[5]),
         pltpu.make_async_copy(nb_hbm.at[0], nb, ld_sem.at[6]),
     ]
-    for load in loads:
-        load.start()
+    for number in (0, 6, 1, 2, 3, 4, 5):
+        loads[number].start()
 
     barrier = pltpu.get_barrier_semaphore()
 
@@ -116,72 +120,102 @@
     def other(step):
         return lax.rem(group + step, jnp.int32(groups)) * pair + core
 
-    def greet_tree(step, carry):
-        greet(lax.rem(tree + step, jnp.int32(trees)), sub)
+    half = max(1, trees // 2)
+
+    def both_ways(reach, action):
+        for there in (-reach, reach):
+            @pl.when((tree + there >= 0) & (tree + there < trees))
+            def _():
+                action(tree + there)
+
+    def partner(core_step):
+        return group * pair + lax.rem(core + core_step, jnp.int32(pair))
+
+    def greet_tree(reach, carry):
+        both_ways(reach, lambda to: greet(to, sub))
         return carry
 
-    lax.fori_loop(1, trees, greet_tree, 0, unroll=trees <= 16)
-    for step in range(1, subs):
-        greet(tree, lax.rem(sub + step, jnp.int32(subs)))
     for slot in (0, 2):
         for step in range(1, groups):
             guarded(
                 goes[slot],
                 functools.partial(lambda sl, st: greet(tree + 1 - sl, other(st)), slot, step),
             )
-    greeted = (trees - 1) + (subs - 1)
+    lax.fori_loop(1, half + 1, greet_tree, 0, unroll=half <= 16)
+    for step in range(1, groups):
+        greet(tree, other(step))
+    for core_step in range(1, pair):
+        greet(tree, partner(core_step))
     sides = goes[0].astype(jnp.int32) + goes[2].astype(jnp.int32)
+    greeted = (pair - 1) + (groups - 1) * (1 + sides)
+    greeted = greeted + jnp.minimum(tree, half) + jnp.minimum(trees - 1 - tree, half)
 
     for slot in (0, 2):
         @pl.when(jnp.logical_not(has[slot]))
         def _():
             win[slot] = jnp.zeros(win.shape[1:], win.dtype)
 
+    loads[6].wait()
+    for j in range(3 * subtree):
+        wanted = (tree - 1) * subtree + j
+        index = jnp.int32(0)
+        alive = jnp.int32(0)
+        for k in range(near):
+            hit = jnp.where(cols_ref[0, k] == wanted, live_ref[0, k], 0)
+            index = index + hit * k
+            alive = alive + hit
+        wown[j] = jnp.where(alive > 0, nb[index], jnp.zeros((leaf, leaf), BF16))
+
     loads[0].wait()
-    pl.semaphore_wait(barrier, greeted + (groups - 1) * sides)
+    pl.semaphore_wait(barrier, greeted)
 
     def spread(slot, step):
         return pltpu.make_async_remote_copy(
-            src_ref=win.at[1, sub],
-            dst_ref=win.at[slot, sub],
+            src_ref=win.at[1, group],
+            dst_ref=win.at[slot, group],
             send_sem=w_send.at[slot, step],
-            recv_sem=w_recv.at[slot, sub],
+            recv_sem=w_recv.at[slot, group],
             device_id=(tree + 1 - slot, other(step)),
             device_id_type=MESH,
         )
 
-    def arrived(slot, from_sub):
+    def arrived(slot, step):
+        held = lax.rem(group + step, jnp.int32(groups))
         pltpu.make_async_remote_copy(
-            src_ref=win.at[slot, from_sub],
-            dst_ref=win.at[slot, from_sub],
-            send_sem=w_send.at[slot, 0],
-            recv_sem=w_recv.at[slot, from_sub],
-            device_id=(tree, sub),
-            device_id_type=MESH,
-        ).wait_recv()
-
-    def hand_over(slot, step, core_step):
-        held = other(step)
-        return pltpu.make_async_remote_copy(
             src_ref=win.at[slot, held],
             dst_ref=win.at[slot, held],
-            send_sem=h_send.at[slot, step, core_step],
+            send_sem=w_send.at[slot, 0],
             recv_sem=w_recv.at[slot, held],
-            device_id=(tree, group * pair + lax.rem(core + core_step, jnp.int32(pair))),
+            device_id=(tree, sub),
+            device_id_type=MESH,
+        ).wait_recv()
+
+    def swap(core_step):
+        return pltpu.make_async_remote_copy(
+            src_ref=wown,
+            dst_ref=wpeer.at[pair - 1 - core_step],
+            send_sem=h_send.at[core_step - 1],
+            recv_sem=h_recv.at[pair - 1 - core_step],
+            device_id=(tree, partner(core_step)),
             device_id_type=MESH,
         )
 
-    first_hops = [(slot, step) for step in range(groups) for slot in (0, 2, 1) if (slot, step) != (1, 0)]
+    first_hops = [(slot, step) for step in range(groups - 1, -1, -1) for slot in (0, 2, 1) if (slot, step) != (1, 0)]
     for slot, step in first_hops:
         guarded(goes[slot], functools.partial(lambda a, b: spread(a, b).start(), slot, step))
     for core_step in range(1, pair):
-        hand_over(1, 0, core_step).start()
+        swap(core_step).start()
+
+    both_ways(
+        half,
+        lambda to: pl.semaphore_signal(known, inc=1, device_id=(to, sub), device_id_type=MESH),
+    )
 
     for load in loads[1:6]:
         load.wait()
     ups = []
     for s in range(subtree):
-        piece = win[1, sub, :, s * leaf : (s + 1) * leaf]
+        piece = win[1, group, :, s * leaf : (s + 1) * leaf]
         ups.append(nt(piece, basis[s]).astype(BF16))
     for number in range(len(levels) - 1):
         start, size = levels[number]
@@ -254,67 +288,53 @@
         far_copy(step).start()
         return carry
 
+    heard = (tree >= half).astype(jnp.int32) + (tree + half < trees).astype(jnp.int32)
+    pl.semaphore_wait(known, heard)
     lax.fori_loop(1, trees, start_far, 0, unroll=trees <= 16)
 
-    loads[6].wait()
-    total = jnp.zeros((subs * own, leaf), F32)
-
-    def relay(slot, step):
-        arrived(slot, other(step))
-        for core_step in range(1, pair):
-            hand_over(slot, step, core_step).start()
-
-    def take(slot, step, core_step):
-        from_core = lax.rem(core + core_step, jnp.int32(pair))
-        arrived(slot, lax.rem(group + step, jnp.int32(groups)) * pair + from_core)
-
-    for slot, step in [(1, step) for step in range(1, groups)] + [
-        (slot, step) for step in range(groups) for slot in (0, 2)
-    ]:
-        guarded(has[slot], functools.partial(relay, slot, step))
-
+    rows = groups * own
+    totals = [jnp.zeros((rows, leaf), F32)] * pair
     for slot in (1, 0, 2):
         for step in range(groups):
+            if (slot, step) != (1, 0):
+                guarded(has[slot], functools.partial(arrived, slot, step))
+        if slot == 1:
             for core_step in range(1, pair):
-                guarded(has[slot], functools.partial(take, slot, step, core_step))
+                swap(core_step).wait_recv()
         for q in range(subtree):
-            wanted = (tree + slot - 1) * subtree + q
-            index = jnp.int32(0)
-            alive = jnp.int32(0)
-            for k in range(near):
-                hit = jnp.where(cols_ref[0, k] == wanted, live_ref[0, k], 0)
-                index = index + hit * k
-                alive = alive + hit
-            piece = win[slot, :, :, q * leaf : (q + 1) * leaf].reshape(subs * own, leaf)
-            total = total + mm(piece, nb[index]) * alive.astype(F32)
-
-    parts = total.reshape(subs, own, leaf).astype(BF16)
-    nsend[...] = parts
-    nrecv[sub] = nsend[sub]
+            piece = win[slot, :, :, q * leaf : (q + 1) * leaf].reshape(rows, leaf)
+            for core_step in range(pair):
+                blocks = wown if core_step == 0 else wpeer.at[core_step - 1]
+                totals[core_step] = totals[core_step] + mm(piece, blocks[slot * subtree + q])
+
+    for core_step in range(pair):
+        leaf_core = lax.rem(core + core_step, jnp.int32(pair))
+        nsend[:, leaf_core] = totals[core_step].reshape(groups, own, leaf).astype(BF16)
+    nrecv[group] = nsend[group]
 
     def near_copy(step):
-        to = lax.rem(sub + step, jnp.int32(subs))
+        to = lax.rem(group + step, jnp.int32(groups))
         return pltpu.make_async_remote_copy(
             src_ref=nsend.at[to],
-            dst_ref=nrecv.at[sub],
+            dst_ref=nrecv.at[group],
             send_sem=n_send.at[to],
-            recv_sem=n_recv.at[sub],
-            device_id=(tree, to),
+            recv_sem=n_recv.at[group],
+            device_id=(tree, other(step)),
             device_id_type=MESH,
         )
 
     def near_arrived(step):
-        source = lax.rem(sub + step, jnp.int32(subs))
+        source = lax.rem(group + step, jnp.int32(groups))
         pltpu.make_async_remote_copy(
             src_ref=nsend.at[source],
             dst_ref=nrecv.at[source],
             send_sem=n_send.at[source],
             recv_sem=n_recv.at[source],
-            device_id=(tree, source),
+            device_id=(tree, other(step)),
             device_id_type=MESH,
         ).wait_recv()
 
-    for step in range(1, subs):
+    for step in range(1, groups):
         near_copy(step).start()
 
     def add_far(step, carry):
@@ -334,27 +354,23 @@
         mm(downs[:, s * rank : (s + 1) * rank].astype(BF16), basis[s]) for s in range(subtree)
     ]
 
-    for step in range(1, subs):
+    for step in range(1, groups):
         near_arrived(step)
     for s in range(subtree):
-        out_ref[:, s * leaf : (s + 1) * leaf] = (nrecv[s].astype(F32) + fars[s]).astype(BF16)
+        near_part = nrecv[s // pair, s % pair].astype(F32)
+        out_ref[:, s * leaf : (s + 1) * leaf] = (near_part + fars[s]).astype(BF16)
 
     for slot, step in first_hops:
         guarded(goes[slot], functools.partial(lambda a, b: spread(a, b).wait_send(), slot, step))
-    for slot in range(3):
-        for step in range(groups):
-            for core_step in range(1, pair):
-                guarded(
-                    has[slot],
-                    functools.partial(lambda *at: hand_over(*at).wait_send(), slot, step, core_step),
-                )
+    for core_step in range(1, pair):
+        swap(core_step).wait_send()
 
     def end_far(step, carry):
         far_copy(step).wait_send()
         return carry
 
     lax.fori_loop(1, trees, end_far, 0, unroll=trees <= 16)
-    for step in range(1, subs):
+    for step in range(1, groups):
         near_copy(step).wait_send()
 
 
@@ -366,6 +382,7 @@
     own, points = vectors.shape
     clusters, far, rank = coupling.shape[:3]
     leaf = leaf_basis.shape[2]
+    window = 3 * leaf_basis.shape[0]
     lanes = -(-clusters * rank // 128) * 128
     any_spec = pl.BlockSpec(memory_space=pl.ANY)
     smem = pl.BlockSpec(memory_space=pltpu.SMEM)
@@ -376,8 +393,10 @@
         in_specs=[any_spec, any_spec, smem, smem] + [any_spec] * 5,
         out_specs=pl.BlockSpec(memory_space=pltpu.VMEM),
         scratch_shapes=[
-            pltpu.VMEM((3, subs, own, points), BF16),
+            pltpu.VMEM((3, groups, own, points), BF16),
             pltpu.VMEM(near_blocks.shape[1:], BF16),
+            pltpu.VMEM((window, leaf, leaf), BF16),
+            pltpu.VMEM((max(1, pair - 1), window, leaf, leaf), BF16),
             pltpu.VMEM(leaf_basis.shape, BF16),
             pltpu.VMEM(transfer.shape, BF16),
             pltpu.VMEM(coupling.shape, BF16),
@@ -386,16 +405,18 @@
             pltpu.VMEM((clusters, far * rank, leaf_basis.shape[0] * rank), BF16),
             pltpu.VMEM((trees, own, lanes), BF16),
             pltpu.VMEM((trees, own, lanes), BF16),
-            pltpu.VMEM((subs, own, leaf), BF16),
-            pltpu.VMEM((subs, own, leaf), BF16),
+            pltpu.VMEM((groups, pair, own, leaf), BF16),
+            pltpu.VMEM((groups, pair, own, leaf), BF16),
+            pltpu.SemaphoreType.REGULAR,
             dma((7,)),
             dma((3, groups)),
-            dma((3, subs)),
-            dma((3, groups, pair)),
+            dma((3, groups)),
+            dma((max(1, pair - 1),)),
+            dma((max(1, pair - 1),)),
             dma((trees,)),
             dma((trees,)),
-            dma((subs,)),
-            dma((subs,)),
+            dma((groups,)),
+            dma((groups,)),
         ],
         compiler_params=pltpu.CompilerParams(collective_id=0, has_side_effects=True),
     )(vectors, near_blocks, near_cols, near_mask, leaf_basis, transfer, coupling, far_targets, far_mask)

time: 16.9 us -> 15.9 us (0.941)
  Pallas kernels: 15.4 us -> 14.3 us
    pallas_call x1, Pallas kernels: 15.4 us -> 14.3 us  [local(): pl.pallas_call(functools.partial(kernel, (trees, subs, pair, chunk)), out...]
where the time goes in v2:
time: 15.9 us; the launch traced here: 15.7 us
  Pallas kernels  14.3 us (90%)
  local copies, waits for them, and re-layouts  1.38 us (9%)
    pallas_call x1, Pallas kernels, local(): pl.pallas_call(functools.partial(kernel, (trees, subs, pair, chunk)), out...  14.3 us
    unnamed x1, local copies, waits for them, and re-layouts  1.38 us

profile of v2, /device:TPU:0, one launch (start us, length us, event | category | flops | bytes accessed | tf_op | source)
XLA Modules:
  0.0 15.7 jit_solution(3439078935952293906)
XLA Ops:
  0.0 14.3 %shard_map.91 = bf16[16,1024]{1,0:T(8,128)(2,1)} custom-call(bf16[16,1024]{1,0:T(8,128)(2,1)} %vec_hbm.1, bf16[1,9,256,256]{3,2,1,0:T(8,128)(2,1)} %nb_hbm.1, s32[1,9]{1,0:T(1,128)} %cols_ref.1, s32[1,9]{1,0:T(1,128)} %live_ref.1, bf16[4,32,256]{2,1,0:T(8,128)(2,1)} %basis_hbm.1, bf16[6,32,32]{2,1,0:T(8,128)(2,1)} %trans_hbm.1, ...), custom_call_target="tpu_custom_call" | custom-call | tf_op jit(solution)/shard_map/pallas_call | solution.py:390
  14.4 1.4 %copy.11 = bf16[16,1024]{1,0:T(8,128)(2,1)} copy(bf16[16,1024]{1,0:T(8,128)(2,1)} %shard_map.91) | data formatting | bytes 65536

commit v3 on v2

--- a/solution.py
+++ b/solution.py
@@ -66,6 +66,7 @@
     coup,
     tgt,
     fmask,
+    dmat,
     rmat,
     fsend,
     frecv,
@@ -166,6 +167,22 @@
             alive = alive + hit
         wown[j] = jnp.where(alive > 0, nb[index], jnp.zeros((leaf, leaf), BF16))
 
+    for load in loads[1:3]:
+        load.wait()
+    dmat[...] = jnp.zeros(dmat.shape, BF16)
+    folded = {s: {s: basis[s]} for s in range(subtree)}
+    for number in range(len(levels) - 1):
+        start, size = levels[number]
+        for kid in range(start, start + size):
+            parent = start + size + (kid - start) // 2
+            for s, block in folded[kid].items():
+                raised = lax.dot_general(
+                    trans[kid], block, (((0,), (0,)), ((), ())), preferred_element_type=F32
+                )
+                folded.setdefault(parent, {})[s] = raised.astype(BF16)
+    for c, blocks in folded.items():
+        for s, block in blocks.items():
+            dmat[c * rank : (c + 1) * rank, s * leaf : (s + 1) * leaf] = block
     loads[0].wait()
     pl.semaphore_wait(barrier, greeted)
 
@@ -190,12 +207,13 @@
             device_id_type=MESH,
         ).wait_recv()
 
-    def swap(core_step):
+    def swap(core_step, slot):
+        part = pl.ds(slot * subtree, subtree)
         return pltpu.make_async_remote_copy(
-            src_ref=wown,
-            dst_ref=wpeer.at[pair - 1 - core_step],
-            send_sem=h_send.at[core_step - 1],
-            recv_sem=h_recv.at[pair - 1 - core_step],
+            src_ref=wown.at[part],
+            dst_ref=wpeer.at[pair - 1 - core_step, part],
+            send_sem=h_send.at[core_step - 1, slot],
+            recv_sem=h_recv.at[pair - 1 - core_step, slot],
             device_id=(tree, partner(core_step)),
             device_id_type=MESH,
         )
@@ -204,24 +222,18 @@
     for slot, step in first_hops:
         guarded(goes[slot], functools.partial(lambda a, b: spread(a, b).start(), slot, step))
     for core_step in range(1, pair):
-        swap(core_step).start()
+        for slot in (1, 0, 2):
+            swap(core_step, slot).start()
 
     both_ways(
         half,
         lambda to: pl.semaphore_signal(known, inc=1, device_id=(to, sub), device_id_type=MESH),
     )
 
-    for load in loads[1:6]:
+    for load in loads[3:6]:
         load.wait()
-    ups = []
-    for s in range(subtree):
-        piece = win[1, group, :, s * leaf : (s + 1) * leaf]
-        ups.append(nt(piece, basis[s]).astype(BF16))
-    for number in range(len(levels) - 1):
-        start, size = levels[number]
-        for parent in range(size // 2):
-            kid = start + 2 * parent
-            ups.append((mm(ups[kid], trans[kid]) + mm(ups[kid + 1], trans[kid + 1])).astype(BF16))
+    lifted = nt(win[1, group], dmat[...]).astype(BF16)
+    ups = [lifted[:, c * rank : (c + 1) * rank] for c in range(clusters)]
 
     wide = far * rank
     targets = tgt[...]
@@ -298,14 +310,13 @@
         for step in range(groups):
             if (slot, step) != (1, 0):
                 guarded(has[slot], functools.partial(arrived, slot, step))
-        if slot == 1:
-            for core_step in range(1, pair):
-                swap(core_step).wait_recv()
-        for q in range(subtree):
-            piece = win[slot, :, :, q * leaf : (q + 1) * leaf].reshape(rows, leaf)
-            for core_step in range(pair):
-                blocks = wown if core_step == 0 else wpeer.at[core_step - 1]
-                totals[core_step] = totals[core_step] + mm(piece, blocks[slot * subtree + q])
+        piece = win[slot].reshape(rows, subtree * leaf)
+        for core_step in range(pair):
+            if core_step > 0:
+                swap(core_step, slot).wait_recv()
+            held = wown if core_step == 0 else wpeer.at[core_step - 1]
+            blocks = held[slot * subtree : (slot + 1) * subtree].reshape(subtree * leaf, leaf)
+            totals[core_step] = totals[core_step] + mm(piece, blocks)
 
     for core_step in range(pair):
         leaf_core = lax.rem(core + core_step, jnp.int32(pair))
@@ -341,29 +352,19 @@
         return carry + frecv[far_arrived(step)].astype(F32)
 
     incoming = lax.fori_loop(1, trees, add_far, fsend[tree].astype(F32), unroll=trees <= 16)
-    downs = incoming[:, levels[-1][0] * rank : clusters * rank]
-    for number in range(len(levels) - 2, -1, -1):
-        start, size = levels[number]
-        pushed = []
-        for parent in range(size // 2):
-            maps = trans[start + 2 * parent : start + 2 * parent + 2].reshape(2 * rank, rank)
-            pushed.append(nt(downs[:, parent * rank : (parent + 1) * rank].astype(BF16), maps))
-        pushed = pushed[0] if len(pushed) == 1 else jnp.concatenate(pushed, axis=1)
-        downs = incoming[:, start * rank : (start + size) * rank] + pushed
-    fars = [
-        mm(downs[:, s * rank : (s + 1) * rank].astype(BF16), basis[s]) for s in range(subtree)
-    ]
+    far_part = mm(incoming.astype(BF16), dmat[...])
 
     for step in range(1, groups):
         near_arrived(step)
     for s in range(subtree):
         near_part = nrecv[s // pair, s % pair].astype(F32)
-        out_ref[:, s * leaf : (s + 1) * leaf] = (near_part + fars[s]).astype(BF16)
+        out_ref[:, s * leaf : (s + 1) * leaf] = (near_part + far_part[:, s * leaf : (s + 1) * leaf]).astype(BF16)
 
     for slot, step in first_hops:
         guarded(goes[slot], functools.partial(lambda a, b: spread(a, b).wait_send(), slot, step))
     for core_step in range(1, pair):
-        swap(core_step).wait_send()
+        for slot in range(3):
+            swap(core_step, slot).wait_send()
 
     def end_far(step, carry):
         far_copy(step).wait_send()
@@ -402,6 +403,7 @@
             pltpu.VMEM(coupling.shape, BF16),
             pltpu.VMEM(far_targets.shape, jnp.int32),
             pltpu.VMEM(far_mask.shape, jnp.int32),
+            pltpu.VMEM((lanes, points), BF16),
             pltpu.VMEM((clusters, far * rank, leaf_basis.shape[0] * rank), BF16),
             pltpu.VMEM((trees, own, lanes), BF16),
             pltpu.VMEM((trees, own, lanes), BF16),
@@ -411,8 +413,8 @@
             dma((7,)),
             dma((3, groups)),
             dma((3, groups)),
-            dma((max(1, pair - 1),)),
-            dma((max(1, pair - 1),)),
+            dma((max(1, pair - 1), 3)),
+            dma((max(1, pair - 1), 3)),
             dma((trees,)),
             dma((trees,)),
             dma((groups,)),

time: 15.9 us -> 15.4 us (0.969)
  Pallas kernels: 14.3 us -> 13.8 us
    pallas_call x1, Pallas kernels: 14.3 us -> 13.8 us  [local(): pl.pallas_call(functools.partial(kernel, (trees, subs, pair, chunk)), out...]
where the time goes in v3:
time: 15.4 us; the launch traced here: 15.2 us
  Pallas kernels  13.8 us (90%)
  local copies, waits for them, and re-layouts  1.38 us (9%)
    pallas_call x1, Pallas kernels, local(): pl.pallas_call(functools.partial(kernel, (trees, subs, pair, chunk)), out...  13.8 us
    unnamed x1, local copies, waits for them, and re-layouts  1.38 us

profile of v3, /device:TPU:0, one launch (start us, length us, event | category | flops | bytes accessed | tf_op | source)
XLA Modules:
  0.0 15.2 jit_solution(2365636773028784816)
XLA Ops:
  0.0 13.8 %shard_map.91 = bf16[16,1024]{1,0:T(8,128)(2,1)} custom-call(bf16[16,1024]{1,0:T(8,128)(2,1)} %vec_hbm.1, bf16[1,9,256,256]{3,2,1,0:T(8,128)(2,1)} %nb_hbm.1, s32[1,9]{1,0:T(1,128)} %cols_ref.1, s32[1,9]{1,0:T(1,128)} %live_ref.1, bf16[4,32,256]{2,1,0:T(8,128)(2,1)} %basis_hbm.1, bf16[6,32,32]{2,1,0:T(8,128)(2,1)} %trans_hbm.1, ...), custom_call_target="tpu_custom_call" | custom-call | tf_op jit(solution)/shard_map/pallas_call | solution.py:391
  13.8 1.4 %copy.11 = bf16[16,1024]{1,0:T(8,128)(2,1)} copy(bf16[16,1024]{1,0:T(8,128)(2,1)} %shard_map.91) | data formatting | bytes 65536
